TPU v7x, 512 devices: a whole 4x4x16 slice. The times are simulated.
512 devices in a mesh: azim: 32 (over z, x_lo), frame: 16 (over x_hi, y, core).
Axes of the slice: x: 4 (x_hi: 2, x_lo: 2; x = x_hi * 2 + x_lo), y: 4, z: 16, core: 2. Of those that a mesh axis runs over, the one named last changes fastest.
Arguments:
- features: bfloat16 [16, 14, 448, 384], P('frame', None, 'azim'), may hold values from -6 to 6
- position_bias: float32 [169, 12], replicated, may hold values from -4 to 4
- attend_weight: bfloat16 [384, 1152], replicated, may hold values from -0.3125 to 0.3125
- output_weight: bfloat16 [384, 384], replicated, may hold values from -0.3125 to 0.3125
- merge_weight: bfloat16 [1536, 768], replicated, may hold values from -0.15625 to 0.15625
- cotangent: bfloat16 [16, 7, 224, 768], P('frame', None, 'azim'), may hold values from -6 to 6
Outputs:
- merged: bfloat16 [16, 7, 224, 768], P('frame', None, 'azim')
- feature_grad: bfloat16 [16, 14, 448, 384], P('frame', None, 'azim')
- attend_grad: float32 [442368], P(('azim', 'frame'))
- output_grad: float32 [147456], P(('azim', 'frame'))
All inputs are finite; a program needn't handle non-finite values.
Results may differ from a plain program's by a relative error of at most 0.0094.
Values may be sent and summed in bfloat16 or wider, within the bound.
A program may use at most 64 MiB of HBM per device.

v0:
```python
import functools

import jax
import jax.numpy as jnp
import ml_dtypes
import numpy as np
from jax import lax
from jax.experimental import pallas as pl
from jax.experimental.pallas import tpu as pltpu
from jax.sharding import Mesh
from jax.sharding import PartitionSpec as P

AZIM = ("azim_0", "azim_1")
AZIM_FRAME = ("azim_0", "azim_1", "frame_0", "frame_1", "frame_2")
FRAME = ("frame_0", "frame_1", "frame_2")

BF = jnp.bfloat16
F32 = jnp.float32
C = 384
OUT = 768
GROUPS = 3
SCALE = 32 ** (-0.5)
WINDOWS = ((0, 1), (1, 1), (0, 0), (1, 0))


def position_row(row, col):
    return 4 * row + col if col < 4 else 32 + 3 * row + col - 4


def east_row(row, col):
    rolled = (row - 3) % 14
    return 32 * (rolled // 7) + 3 * (rolled % 7) + col


@functools.cache
def tables():
    to_window = np.zeros((256, 224), np.float32)
    for a in range(2):
        for b in range(2):
            for row in range(7):
                for col in range(7):
                    frame_row, frame_col = (7 * a + row + 3) % 14, 7 * b + col + 3
                    if frame_col >= 14:
                        continue
                    at = position_row(row, col)
                    line = 64 * a + at if b == 0 else 128 + 32 * a + at
                    to_window[line, 16 * frame_row + frame_col] = 1
    for row in range(14):
        for col in range(3):
            to_window[192 + east_row(row, col), 16 * row + col] = 1
    to_quad = np.zeros((256, 224), np.float32)
    for block in range(4):
        for i in range(7):
            for j in range(7):
                token = 16 * (2 * i + block % 2) + 2 * j + block // 2
                to_quad[64 * block + 8 * i + j, token] = 1
    window_to_quad = to_quad @ to_window.T
    rows = np.zeros((C, C), np.float32)
    for c in range(2):
        for xi in range(4):
            for k in range(3):
                for z in range(16):
                    rows[192 * c + 48 * xi + 16 * k + z, 24 * z + 6 * xi + 3 * c + k] = 1
    index = np.full((64, 64), 255.0, np.float32)
    mask = np.zeros((2, 64, 64), np.float32)
    valid = np.zeros(64, bool)
    for row in range(7):
        for col in range(7):
            p = position_row(row, col)
            valid[p] = True
            for row_q in range(7):
                for col_q in range(7):
                    q = position_row(row_q, col_q)
                    index[p, q] = 13 * (row - row_q + 6) + col - col_q + 6
                    if (row < 4) != (row_q < 4):
                        mask[1, p, q] = -100.0
    mask[:, :, ~valid] = -1e30
    mask = np.concatenate([mask, mask], -1)
    bf = ml_dtypes.bfloat16
    return (
        to_window.astype(bf),
        np.ascontiguousarray(to_window.T).astype(bf),
        to_quad.astype(bf),
        np.ascontiguousarray(to_quad.T).astype(bf),
        window_to_quad.astype(bf),
        np.ascontiguousarray(window_to_quad.T).astype(bf),
        rows.astype(bf),
        index.reshape(32, 128),
        mask,
    )


def mm(left, right):
    return lax.dot_general(left, right, (((1,), (0,)), ((), ())), preferred_element_type=F32)


def mm_t(left, right):
    return lax.dot_general(left, right, (((1,), (1,)), ((), ())), preferred_element_type=F32)


def t_mm(left, right):
    return lax.dot_general(left, right, (((0,), (0,)), ((), ())), preferred_element_type=F32)


def normalize(values):
    centred = values - jnp.mean(values, -1, keepdims=True)
    inverse_std = lax.rsqrt(jnp.mean(centred * centred, -1, keepdims=True) + 1e-05)
    return centred * inverse_std, inverse_std


def normalize_back(normed, inverse_std, grads):
    first = jnp.mean(grads, -1, keepdims=True)
    second = jnp.mean(grads * normed, -1, keepdims=True)
    return inverse_std * (grads - first - normed * second)


def window_of(values, a, b):
    if b == 0:
        return values[64 * a : 64 * a + 64]
    near, far = 128 + 32 * a, 192 + 32 * a
    return jnp.concatenate([values[near : near + 32], values[far : far + 32]], 0)


def put_window(ref, a, b, lanes, values):
    if b == 0:
        ref[64 * a : 64 * a + 64, lanes] = values
    else:
        near, far = 128 + 32 * a, 192 + 32 * a
        ref[near : near + 32, lanes] = values[:32]
        ref[far : far + 32, lanes] = values[32:]


def get_window(ref, a, b, lanes):
    if b == 0:
        return ref[64 * a : 64 * a + 64, lanes]
    near, far = 128 + 32 * a, 192 + 32 * a
    return jnp.concatenate([ref[near : near + 32, lanes], ref[far : far + 32, lanes]], 0)


def halves(op, empty, low, values):
    first = op(jnp.where(low, values, empty), -1, keepdims=True)
    second = op(jnp.where(low, empty, values), -1, keepdims=True)
    return jnp.where(low, first, second)


NAMES = (
    "feat", "cot", "pos", "w_attend", "w_out", "w_merge", "to_window", "to_window_t", "to_quad",
    "to_quad_t", "win_quad", "win_quad_t", "row_pick", "index", "mask",
)
ORDER = (
    "feat", "to_window", "w_attend", "pos", "index", "mask", "cot", "w_merge", "row_pick",
    "to_quad", "win_quad", "w_out", "win_quad_t", "to_quad_t", "to_window_t",
)
N_IN = len(NAMES)


def kernel(scatter, *refs):
    given, refs = refs[:N_IN], refs[N_IN:]
    merged_ref, grad_ref, share_ref = refs[:3]
    if scatter:
        refs = refs[3:]
    else:
        local_ref, refs = refs[3], refs[4:]
    held, refs = refs[:N_IN], refs[N_IN:]
    (
        x_scr, cot_scr, table_scr, bias_a, bias_b, normed_scr, std_scr,
        normed_east, std_east, qkv, probs, attended, branch_grad, outer, proj_grad,
        hidden_grad, left_o, left_r, feature_scr,
        ex_send, ex_recv,
        g_own, g_send, g_recv, x_own, x_send, x_recv, y_send, y_recv, z_line, z_send, z_recv,
        in_sem, ex_ssem, ex_rsem, c_ssem, c_rsem, x_ssem, x_rsem, y_ssem, y_rsem,
        z_ssem, z_rsem, near_sem,
    ) = refs
    (
        feat, cot, pos, w_attend, w_out, w_merge, to_window, to_window_t, to_quad, to_quad_t,
        win_quad, win_quad_t, row_pick, index, mask,
    ) = held
    copies = {
        name: pltpu.make_async_copy(given[i], held[i], in_sem.at[i])
        for i, name in enumerate(NAMES)
    }
    for name in ORDER:
        copies[name].start()

    z, x_lo = lax.axis_index("azim_0"), lax.axis_index("azim_1")
    x_hi, y, core = (lax.axis_index(name) for name in FRAME)
    n_z = lax.axis_size("azim_0")
    n_azim = n_z * 2
    azim = 2 * z + x_lo
    east, west = (azim + 1) % n_azim, (azim + n_azim - 1) % n_azim
    east_id = {"azim_0": east // 2, "azim_1": east % 2}
    west_id = {"azim_0": west // 2, "azim_1": west % 2}
    xi = 2 * x_lo + x_hi

    def x_id(step):
        other = (xi + step) % 4
        return {"azim_1": other // 2, "frame_0": other % 2}

    def z_id(step):
        return {"azim_0": (z + n_z + step) % n_z}

    barrier = pltpu.get_barrier_semaphore()
    near = [east_id, west_id]
    if scatter:
        near += [{"frame_2": 1 - core}]
        near += [x_id(step) for step in (1, 2, 3)]
        near += [{"frame_1": (y + step) % 4} for step in (1, 2, 3)]
        near += [{"frame_1": (y + step) % 4, "frame_2": 1 - core} for step in (1, 2, 3)]
        near += [z_id(1), z_id(-1)]
    for device in near:
        pl.semaphore_signal(barrier, inc=1, device_id=device)

    def exchange(i, device):
        return pltpu.make_async_remote_copy(
            src_ref=ex_send.at[i], dst_ref=ex_recv.at[i], send_sem=ex_ssem.at[i],
            recv_sem=ex_rsem.at[i], device_id=device,
        )

    copies["feat"].wait()
    x_scr[...] = jnp.zeros_like(x_scr)
    for row in range(14):
        x_scr[row, 0:14, :] = feat[row].astype(F32)
    tokens = x_scr[...].reshape(224, C)
    tokens16 = tokens.astype(BF)
    copies["to_window"].wait()
    ex_send[0] = mm(to_window[192:256], tokens16).astype(BF)
    pl.semaphore_wait(barrier, len(near))
    exchange(0, west_id).start()
    if scatter:
        for step in (1, -1):
            pl.semaphore_signal(near_sem.at[0], inc=1, device_id=z_id(step))

    def widen_reach(i):
        if not scatter:
            return
        pl.semaphore_wait(near_sem.at[i], 2)
        if i < 2:
            for step in (2 ** (i + 1), -(2 ** (i + 1))):
                pl.semaphore_signal(near_sem.at[i + 1], inc=1, device_id=z_id(step))

    normed, inverse_std = normalize(tokens)
    normed_scr[...] = normed
    std_scr[...] = inverse_std
    rolled_own = mm(to_window[0:192], normed.astype(BF)).astype(BF)
    copies["w_attend"].wait()
    qkv[0:192] = mm(rolled_own, w_attend[...]).astype(BF)

    copies["pos"].wait()
    copies["index"].wait()
    copies["mask"].wait()
    table_scr[...] = jnp.zeros_like(table_scr)
    table_scr[0:12, 0:169] = pos[...]
    table = table_scr[...]
    high = table.astype(BF).astype(F32)
    both = jnp.concatenate([high, table - high], 0).astype(BF)
    lane = lax.broadcasted_iota(jnp.int32, (1, 128), 1)
    entry = lax.broadcasted_iota(jnp.int32, (256, 128), 0).astype(F32)
    for t in range(0, 32, 4):
        picks = [
            jnp.where(entry == index[u : u + 1, :], 1.0, 0.0).astype(BF) for u in range(t, t + 4)
        ]
        wide = mm(both, jnp.concatenate(picks, 1))
        for u in range(4):
            part = wide[:, 128 * u : 128 * u + 128]
            part = part[0:16] + part[16:32]
            turned = pltpu.roll(part, 64, 1)
            p = 2 * (t + u)
            bias_a[pl.ds(p, 16, stride=64), :] = part
            bias_a[pl.ds(p + 1, 16, stride=64), :] = turned
            bias_b[pl.ds(p, 16, stride=64), :] = turned
            bias_b[pl.ds(p + 1, 16, stride=64), :] = part
    low = lane < 64

    def pair_bias(pair):
        first = bias_a[128 * pair : 128 * pair + 64, :]
        second = bias_b[128 * pair + 64 : 128 * pair + 128, :]
        return jnp.where(low, first, second)

    copies["cot"].wait()
    cot_scr[...] = jnp.zeros_like(cot_scr)
    for row in range(7):
        cot_scr[row, 0:7, :] = cot[row].astype(F32)
    copies["w_merge"].wait()
    quad_grad_in = mm_t(cot_scr[...].reshape(64, OUT).astype(BF), w_merge[...])

    exchange(0, west_id).wait()
    widen_reach(0)
    normed, inverse_std = normalize(ex_recv[0].astype(F32))
    normed_east[...] = normed
    std_east[...] = inverse_std
    rolled_east = normed.astype(BF)
    qkv[192:256] = mm(rolled_east, w_attend[...]).astype(BF)

    head_lanes = [(lane // 32 == h).astype(F32).astype(BF) for h in range(4)]

    def spread(block):
        return jnp.concatenate([block * head_lanes[h] for h in range(4)], 0)

    def heads_of(wide):
        total = wide[0:64] * head_lanes[0].astype(F32)
        for h in range(1, 4):
            total = total + wide[64 * h : 64 * h + 64] * head_lanes[h].astype(F32)
        return total

    def group_lanes(kind, group):
        start = C * kind + 128 * group
        return slice(start, start + 128)

    def units_of(windows):
        return [(w, group) for w in windows for group in range(GROUPS)]

    def of_window(ref, w, kind, group):
        return get_window(ref, *WINDOWS[w], group_lanes(kind, group))

    ones = (lax.broadcasted_iota(jnp.int32, (128, 128), 0) < 64) == low
    ones = ones.astype(F32).astype(BF)

    def half_sums(values):
        joined = jnp.concatenate(values, 0)
        high = joined.astype(BF)
        rest = (joined - high.astype(F32)).astype(BF)
        total = mm(high, ones) + mm(rest, ones)
        return [total[64 * i : 64 * i + 64] for i in range(len(values))]

    def split_halves(wide):
        return [part[:, 128 * i : 128 * i + 128] for part in wide for i in range(2)]

    def join_halves(parts):
        return [
            jnp.concatenate([parts[i].astype(BF), parts[i + 1].astype(BF)], 1)
            for i in range(0, len(parts), 2)
        ]

    def attend(*windows):
        units = units_of(windows)
        scores = [
            mm_t(of_window(qkv, w, 0, g), spread(of_window(qkv, w, 1, g))) for w, g in units
        ]
        parts = split_halves(scores)
        for i, (w, g) in enumerate(units):
            for j in range(2):
                bias = pair_bias(2 * g + j) + mask[WINDOWS[w][0]]
                parts[2 * i + j] = parts[2 * i + j] * SCALE + bias
        tops = [halves(jnp.max, -3e38, low, part) for part in parts]
        parts = [jnp.exp(part - top) for part, top in zip(parts, tops)]
        sums = half_sums(parts)
        parts = [part * (1.0 / total) for part, total in zip(parts, sums)]
        for i, (w, g) in enumerate(units):
            for j in range(2):
                probs[GROUPS * w + g, :, 128 * j : 128 * j + 128] = parts[2 * i + j]
        for (w, g), prob in zip(units, join_halves(parts)):
            result = mm(prob, spread(of_window(qkv, w, 2, g))).astype(BF)
            put_window(attended, *WINDOWS[w], group_lanes(0, g), result)

    attend(0, 1)
    ex_send[1] = attended[192:256]
    exchange(1, east_id).start()
    attend(2, 3)
    copies["row_pick"].wait()
    left_r[:, 0:192] = mm_t(row_pick[...], rolled_own).astype(BF)
    left_r[:, 192:256] = mm_t(row_pick[...], rolled_east).astype(BF)
    left_o[...] = mm_t(row_pick[...], attended[...]).astype(BF)
    copies["to_quad"].wait()
    copies["win_quad"].wait()
    copies["w_out"].wait()
    features_quad = mm(to_quad[...], tokens16)
    exchange(1, east_id).wait()
    widen_reach(1)

    extended = jnp.concatenate([attended[0:192], ex_recv[1]], 0)
    attended_quad = mm(win_quad[...], extended).astype(BF)
    hidden = (features_quad + mm(attended_quad, w_out[...])).astype(BF).astype(F32)
    quads = [hidden[64 * e : 64 * e + 64] for e in range(4)]

    def mean(blocks):
        total = (blocks[0] + blocks[1]) + (blocks[2] + blocks[3])
        return jnp.sum(total, -1, keepdims=True) * (1.0 / (4 * C))

    centre = mean(quads)
    quads = [quad - centre for quad in quads]
    quad_std = lax.rsqrt(mean([quad * quad for quad in quads]) + 1e-05)
    quads = [quad * quad_std for quad in quads]
    grads = [quad_grad_in[:, C * e : C * e + C] for e in range(4)]
    first = mean(grads)
    second = mean([grad * quad for grad, quad in zip(grads, quads)])
    for e in range(4):
        value = quad_std * (grads[e] - first - quads[e] * second)
        hidden_grad[64 * e : 64 * e + 64] = value.astype(BF)
    copies["win_quad_t"].wait()
    ex_send[2] = mm(win_quad_t[192:256], hidden_grad[...]).astype(BF)
    exchange(2, west_id).start()
    own_grad = mm(win_quad_t[0:192], hidden_grad[...]).astype(BF)
    branch_grad[0:192] = own_grad
    outer[0:192] = mm_t(own_grad, w_out[...]).astype(BF)
    merged = mm(jnp.concatenate([quad.astype(BF) for quad in quads], 1), w_merge[...])
    for i in range(7):
        merged_ref[i] = merged[8 * i : 8 * i + 7].astype(BF)
    copies["to_quad_t"].wait()
    hidden_own = mm(to_quad_t[...], hidden_grad[...])

    def values_back(*windows):
        units = units_of(windows)
        wide = [
            t_mm(probs[GROUPS * w + g].astype(BF), of_window(outer, w, 0, g)) for w, g in units
        ]
        for (w, g), value in zip(units, wide):
            back = heads_of(value).astype(BF)
            put_window(proj_grad, *WINDOWS[w], group_lanes(2, g), back)

    def scores_back(*windows):
        units = units_of(windows)
        wide = [
            mm_t(of_window(outer, w, 0, g), spread(of_window(qkv, w, 2, g))) for w, g in units
        ]
        grads = split_halves(wide)
        prob = split_halves([probs[GROUPS * w + g] for w, g in units])
        sums = half_sums([p * grad for p, grad in zip(prob, grads)])
        parts = [p * (grad - total) * SCALE for p, grad, total in zip(prob, grads, sums)]
        soft = join_halves(parts)
        wide = [t_mm(part, of_window(qkv, w, 0, g)) for (w, g), part in zip(units, soft)]
        for (w, g), part in zip(units, soft):
            back = mm(part, spread(of_window(qkv, w, 1, g))).astype(BF)
            put_window(proj_grad, *WINDOWS[w], group_lanes(0, g), back)
        for (w, g), value in zip(units, wide):
            back = heads_of(value).astype(BF)
            put_window(proj_grad, *WINDOWS[w], group_lanes(1, g), back)

    def core_copy(i):
        return pltpu.make_async_remote_copy(
            src_ref=g_send.at[i, 1 - core], dst_ref=g_recv.at[i], send_sem=c_ssem.at[i],
            recv_sem=c_rsem.at[i], device_id={"frame_2": 1 - core},
        )

    def start_core(i, product):
        product = product.reshape(2, 192, C)
        g_own[i] = product
        if scatter:
            g_send[i] = product.astype(BF)
            core_copy(i).start()

    def x_copy(i, step):
        return pltpu.make_async_remote_copy(
            src_ref=x_send.at[i, (xi + step) % 4], dst_ref=x_recv.at[i, step - 1],
            send_sem=x_ssem.at[i, step - 1], recv_sem=x_rsem.at[i, step - 1],
            device_id=x_id(step),
        )

    def start_x(i):
        if not scatter:
            return
        core_copy(i).wait()
        total = (g_own[i, core] + g_recv[i].astype(F32)).reshape(4, 48, C)
        x_own[i] = total
        x_send[i] = total.astype(BF)
        for step in (2, 1, 3):
            x_copy(i, step).start()

    def end_x(i):
        for step in (1, 2, 3):
            x_copy(i, step).wait()
        total = x_own[i, xi]
        for step in (1, 2, 3):
            total = total + x_recv[i, step - 1].astype(F32)
        return total

    scores_back(2, 3)
    exchange(2, west_id).wait()
    widen_reach(2)
    branch_grad[192:256] = ex_recv[2]
    outer[192:256] = mm_t(ex_recv[2], w_out[...]).astype(BF)
    start_core(0, mm(left_o[...], branch_grad[...]))
    values_back(0, 1, 2, 3)
    start_core(1, mm(left_r[...], proj_grad[:, 2 * C : 3 * C]))
    start_x(0)
    scores_back(0, 1)
    start_x(1)
    start_core(2, mm(left_r[...], proj_grad[:, 0:C]))
    start_core(3, mm(left_r[...], proj_grad[:, C : 2 * C]))
    east_grad = mm_t(proj_grad[192:256], w_attend[...])
    east_grad = normalize_back(normed_east[...], std_east[...], east_grad)
    ex_send[3] = east_grad.astype(BF)
    exchange(3, east_id).start()
    start_x(2)
    start_x(3)
    copies["to_window_t"].wait()
    own_proj = mm(to_window_t[:, 0:192], proj_grad[0:192]).astype(BF)
    own_grad = mm_t(own_proj, w_attend[...])
    own_grad = normalize_back(normed_scr[...], std_scr[...], own_grad)
    feature_scr[...] = hidden_own + own_grad

    def end_features():
        exchange(3, east_id).wait()
        grad = feature_scr[...] + mm(to_window_t[:, 192:256], ex_recv[3])
        grad = grad.reshape(14, 16, C)
        for row in range(14):
            grad_ref[row] = grad[row, 0:14].astype(BF)

    if not scatter:
        end_features()
        share_ref[...] = jnp.zeros_like(share_ref)
        local_ref[...] = g_own[...]
        return

    output_sum, values_sum = end_x(0), end_x(1)
    queries_sum, keys_sum = end_x(2), end_x(3)
    joined = jnp.concatenate([queries_sum, keys_sum, values_sum], 1)
    quarters = [
        joined[:, 0:384],
        pltpu.roll(joined[:, 256:768], 512 - 32, 1)[:, 0:384],
        pltpu.roll(joined[:, 512:1024], 512 - 64, 1)[:, 0:384],
        pltpu.roll(joined[:, 768:1152], 384 - 96, 1),
    ]
    pieces = [
        output_sum[:, 0:128],
        pltpu.roll(output_sum[:, 0:256], 256 - 96, 1)[:, 0:128],
        pltpu.roll(output_sum[:, 128:384], 256 - 64, 1)[:, 0:128],
        pltpu.roll(output_sum[:, 256:384], 128 - 32, 1),
    ]
    for m in range(4):
        for i in range(3):
            k, t = divmod(3 * m + i, 4)
            rows = slice(16 * k, 16 * k + 16)
            y_send[m, :, 384 * i : 384 * i + 384] = quarters[t][rows].astype(BF)
            lanes = slice(1152 + 128 * i, 1280 + 128 * i)
            y_send[m, :, lanes] = pieces[t][rows].astype(BF)

    def y_copy(m):
        return pltpu.make_async_remote_copy(
            src_ref=y_send.at[m], dst_ref=y_recv.at[y], send_sem=y_ssem.at[m],
            recv_sem=y_rsem.at[y],
            device_id={"frame_1": 2 * core + m // 2, "frame_2": m % 2},
        )

    def y_landed(source):
        return pltpu.make_async_remote_copy(
            src_ref=y_send.at[0], dst_ref=y_recv.at[source], send_sem=y_ssem.at[0],
            recv_sem=y_rsem.at[source], device_id={"frame_2": 1 - core},
        )

    for m in range(4):
        mine = jnp.logical_and(2 * core + m // 2 == y, core == m % 2)

        @pl.when(mine)
        def _():
            y_recv[y] = y_send[m]

        @pl.when(jnp.logical_not(mine))
        def _():
            y_copy(m).start()

    for source in range(4):
        mine = jnp.logical_and(y == source, y // 2 == core)

        @pl.when(jnp.logical_not(mine))
        def _():
            y_landed(source).wait_recv()

    total = y_recv[0].astype(F32)
    for source in range(1, 4):
        total = total + y_recv[source].astype(F32)
    for t in range(12):
        z_line[pl.ds(t, 16, stride=16), :] = total[:, 128 * t : 128 * t + 128]
    for t in range(12, 16):
        z_line[pl.ds(t, 16, stride=16), :] = jnp.zeros((16, 128), F32)
    z_send[...] = z_line[...].reshape(16, 16, 128).astype(BF)

    def z_copy(step):
        return pltpu.make_async_remote_copy(
            src_ref=z_send.at[(z + step) % 16], dst_ref=z_recv.at[step - 1],
            send_sem=z_ssem.at[step - 1], recv_sem=z_rsem.at[step - 1], device_id=z_id(step),
        )

    steps = sorted(range(1, 16), key=lambda step: -min(step, 16 - step))
    for step in steps:
        z_copy(step).start()
    end_features()
    for m in range(4):
        mine = jnp.logical_and(2 * core + m // 2 == y, core == m % 2)

        @pl.when(jnp.logical_not(mine))
        def _():
            y_copy(m).wait_send()

    total = z_send[z].astype(F32)
    for step in steps[::-1]:
        z_copy(step).wait()
        total = total + z_recv[step - 1].astype(F32)
    share_ref[...] = total


def finish(merged_in, grad_in, share, merged_ref, grad_ref, attend_ref, output_ref):
    merged_ref[0] = merged_in[...]
    grad_ref[0] = grad_in[...]
    lane = lax.broadcasted_iota(jnp.int32, (1, 128), 1)

    def row(i, turn=0):
        value = share[i : i + 1, :]
        return pltpu.roll(value, turn, 1) if turn else value

    one = [row(i, 32) for i in (3, 4, 5)]
    two = [row(i, 64) for i in (6, 7, 8)]
    low, half = lane < 32, lane < 64
    attend = [
        row(0),
        row(1),
        jnp.where(low, row(2), one[0]),
        jnp.where(low, one[0], one[1]),
        jnp.where(low, one[1], jnp.where(half, one[2], two[0])),
        jnp.where(half, two[0], two[1]),
        jnp.where(half, two[1], two[2]),
    ]
    middle, last = row(10, 96), row(11, 64)
    output = [jnp.where(lane < 96, row(9), middle), jnp.where(half, middle, last), last]
    for ref, rows in ((attend_ref, attend), (output_ref, output)):
        for i, value in enumerate(rows):
            count = min(128, ref.shape[0] - 128 * i)
            ref[128 * i : 128 * i + count] = value.reshape(128)[:count]


def local_call(scatter, features, position_bias, attend_weight, output_weight, merge_weight, cotangent):
    given = (features[0], cotangent[0], position_bias.T, attend_weight, output_weight, merge_weight)
    given = given + tuple(jnp.asarray(table) for table in tables())
    dma = pltpu.SemaphoreType.DMA
    scratch = [pltpu.VMEM(a.shape, a.dtype) for a in given]
    scratch += [
        pltpu.VMEM((14, 16, C), F32),
        pltpu.VMEM((8, 8, OUT), F32),
        pltpu.VMEM((16, 256), F32),
        pltpu.VMEM((1024, 128), F32),
        pltpu.VMEM((1024, 128), F32),
        pltpu.VMEM((224, C), F32),
        pltpu.VMEM((224, 1), F32),
        pltpu.VMEM((64, C), F32),
        pltpu.VMEM((64, 1), F32),
        pltpu.VMEM((256, 3 * C), BF),
        pltpu.VMEM((12, 64, 256), F32),
        pltpu.VMEM((256, C), BF),
        pltpu.VMEM((256, C), BF),
        pltpu.VMEM((256, C), BF),
        pltpu.VMEM((256, 3 * C), BF),
        pltpu.VMEM((256, C), BF),
        pltpu.VMEM((C, 256), BF),
        pltpu.VMEM((C, 256), BF),
        pltpu.VMEM((224, C), F32),
        pltpu.VMEM((4, 64, C), BF),
        pltpu.VMEM((4, 64, C), BF),
        pltpu.VMEM((4, 2, 192, C), F32),
        pltpu.VMEM((4, 2, 192, C), BF),
        pltpu.VMEM((4, 192, C), BF),
        pltpu.VMEM((4, 4, 48, C), F32),
        pltpu.VMEM((4, 4, 48, C), BF),
        pltpu.VMEM((4, 3, 48, C), BF),
        pltpu.VMEM((4, 16, 1536), BF),
        pltpu.VMEM((4, 16, 1536), BF),
        pltpu.VMEM((256, 128), F32),
        pltpu.VMEM((16, 16, 128), BF),
        pltpu.VMEM((15, 16, 128), BF),
        dma((N_IN,)), dma((4,)), dma((4,)), dma((4,)), dma((4,)), dma((4, 3)), dma((4, 3)),
        dma((4,)), dma((4,)), dma((15,)), dma((15,)), pltpu.SemaphoreType.REGULAR((3,)),
    ]
    vmem = pl.BlockSpec(memory_space=pltpu.VMEM)
    return pl.pallas_call(
        functools.partial(kernel, scatter),
        out_shape=(
            jax.ShapeDtypeStruct((7, 7, OUT), BF),
            jax.ShapeDtypeStruct((14, 14, C), BF),
            jax.ShapeDtypeStruct((16, 128), F32),
        )
        + (() if scatter else (jax.ShapeDtypeStruct((4, 2, 192, C), F32),)),
        in_specs=[pl.BlockSpec(memory_space=pl.ANY)] * N_IN,
        out_specs=(vmem,) * (3 if scatter else 4),
        scratch_shapes=scratch,
        compiler_params=pltpu.CompilerParams(collective_id=0, has_side_effects=True),
    )(*given)


def per_device(*arrays):
    merged, feature_grad, share = local_call(True, *arrays)
    vmem = pl.BlockSpec(memory_space=pltpu.VMEM)
    return pl.pallas_call(
        finish,
        out_shape=(
            jax.ShapeDtypeStruct((1, *merged.shape), BF),
            jax.ShapeDtypeStruct((1, *feature_grad.shape), BF),
            jax.ShapeDtypeStruct((864,), F32),
            jax.ShapeDtypeStruct((288,), F32),
        ),
        in_specs=(vmem,) * 3,
        out_specs=(vmem,) * 4,
    )(merged, feature_grad, share)


def solution(mesh):
    split = Mesh(mesh.devices.reshape(16, 2, 2, 4, 2), AZIM_FRAME)
    placed = (P(FRAME, None, AZIM, None), P(), P(), P(), P(), P(FRAME, None, AZIM, None))
    return jax.shard_map(
        per_device,
        mesh=split,
        in_specs=placed,
        out_specs=(
            P(FRAME, None, AZIM, None),
            P(FRAME, None, AZIM, None),
            P(AZIM_FRAME),
            P(AZIM_FRAME),
        ),
        check_vma=False,
    )
```

profile of v0, /device:TPU:1, one launch (start us, length us, event | category | flops | bytes accessed | tf_op | source)
XLA Modules:
  0.0 54.6 jit_solution(17100573928363937052)
XLA Ops:
  0.6 52.3 %shard_map.174 = (bf16[7,7,768]{2,1,0:T(8,128)(2,1)}, bf16[14,14,384]{2,1,0:T(8,128)(2,1)}, f32[16,128]{1,0:T(8,128)}) custom-call(bf16[14,14,384]{2,1,0:T(8,128)(2,1)} %bitcast.3, bf16[7,7,768]{2,1,0:T(8,128)(2,1)} %bitcast.4, f32[12,169]{1,0:T(8,128)} %bitcast.5, bf16[384,1152]{1,0:T(8,128)(2,1)} %refs_3_.1, bf16[384,384]{1,0:T(8,128)(2,1)} %refs_4_.1, ...), custom_call_target="tpu_custom_call" | custom-call | tf_op jit(solution)/shard_map/pallas_call | solution.py:662
  52.9 1.7 %shard_map.175 = (bf16[1,7,7,768]{3,2,1,0:T(8,128)(2,1)}, bf16[1,14,14,384]{3,2,1,0:T(8,128)(2,1)}, f32[864]{0:T(1024)}, f32[288]{0:T(512)}) custom-call(bf16[7,7,768]{2,1,0:T(8,128)(2,1)} %get-tuple-element.7.merged_in, bf16[14,14,384]{2,1,0:T(8,128)(2,1)} %get-tuple-element.8.grad_in, f32[16,128]{1,0:T(8,128)} %get-tuple-element.9.share), custom_call_target="tpu_custom_call" | custom-call | tf_op jit(solution)/shard_map/pallas_call | solution.py:680
where the time goes:
time: 54.9 us; the launch traced here: 54.6 us
  Pallas kernels  54 us (98%)
  between operations  0.64 us (1%)
    pallas_call x1, Pallas kernels, local_call(): pl.pallas_call(functools.partial(kernel, scatter), out_shape=(jax.ShapeDt...  52.3 us
    pallas_call x1, Pallas kernels, per_device(): pl.pallas_call(finish, out_shape=(jax.ShapeDtypeStruct((1, *merged.shape)...  1.69 us

commit v1 on v0

--- a/solution.py
+++ b/solution.py
@@ -167,7 +167,8 @@
         normed_east, std_east, qkv, probs, attended, branch_grad, outer, proj_grad,
         hidden_grad, left_o, left_r, feature_scr,
         ex_send, ex_recv,
-        g_own, g_send, g_recv, x_own, x_send, x_recv, y_send, y_recv, z_line, z_send, z_recv,
+        g_own, g_send, g_recv, x_own, x_send, x_recv, y_send, y_recv,
+        x_own2, x_send2, x_recv2, y_send2, y_recv2, z_line, z_send, z_recv,
         in_sem, ex_ssem, ex_rsem, c_ssem, c_rsem, x_ssem, x_rsem, y_ssem, y_rsem,
         z_ssem, z_rsem, near_sem,
     ) = refs
@@ -438,30 +439,147 @@
             g_send[i] = product.astype(BF)
             core_copy(i).start()
 
-    def x_copy(i, step):
+    def x_copies(i, sent, landing):
+        return [
+            pltpu.make_async_remote_copy(
+                src_ref=sent.at[(xi + step) % 4], dst_ref=landing.at[step - 1],
+                send_sem=x_ssem.at[i, step - 1], recv_sem=x_rsem.at[i, step - 1],
+                device_id=x_id(step),
+            )
+            for step in (2, 1, 3)
+        ]
+
+    def y_copy(i, m, sent, landing):
         return pltpu.make_async_remote_copy(
-            src_ref=x_send.at[i, (xi + step) % 4], dst_ref=x_recv.at[i, step - 1],
-            send_sem=x_ssem.at[i, step - 1], recv_sem=x_rsem.at[i, step - 1],
-            device_id=x_id(step),
+            src_ref=sent.at[m], dst_ref=landing.at[y], send_sem=y_ssem.at[i, m],
+            recv_sem=y_rsem.at[i, y],
+            device_id={"frame_1": 2 * core + m // 2, "frame_2": m % 2},
         )
 
-    def start_x(i):
+    def y_landed(i, source, sent, landing):
+        return pltpu.make_async_remote_copy(
+            src_ref=sent.at[0], dst_ref=landing.at[source], send_sem=y_ssem.at[i, 0],
+            recv_sem=y_rsem.at[i, source], device_id={"frame_2": 1 - core},
+        )
+
+    def stays(m):
+        return jnp.logical_and(2 * core + m // 2 == y, core == m % 2)
+
+    def start_y(i, sent, landing):
+        for m in range(4):
+
+            @pl.when(stays(m))
+            def _():
+                landing[y] = sent[m]
+
+            @pl.when(jnp.logical_not(stays(m)))
+            def _():
+                y_copy(i, m, sent, landing).start()
+
+    def end_y(i, sent, landing):
+        for source in range(4):
+            mine = jnp.logical_and(y == source, y // 2 == core)
+
+            @pl.when(jnp.logical_not(mine))
+            def _():
+                y_landed(i, source, sent, landing).wait_recv()
+
+        for m in range(4):
+
+            @pl.when(jnp.logical_not(stays(m)))
+            def _():
+                y_copy(i, m, sent, landing).wait_send()
+
+        total = landing[0].astype(F32)
+        for source in range(1, 4):
+            total = total + landing[source].astype(F32)
+        return total
+
+    wide_lane = lax.broadcasted_iota(jnp.int32, (1, C), 1)
+
+    def segments(i, block):
+        one, two, three = (block[16 * k : 16 * k + 16] for k in range(3))
+
+        def left(value, count):
+            return pltpu.roll(value, C - count, 1)
+
+        if i == 0:
+            second = jnp.where(wide_lane < 96, left(one, 288), pltpu.roll(two, 96, 1))
+            third = jnp.where(wide_lane < 192, left(two, 192), pltpu.roll(three, 192, 1))
+            return one, second, third, left(three, 96)
+        if i == 1:
+            return one, left(one, 96), two, three
+        if i == 2:
+            return one, two, three, left(three, 288)
+        return one, two, left(two, 192), three
+
+    def start_first(i):
         if not scatter:
             return
         core_copy(i).wait()
         total = (g_own[i, core] + g_recv[i].astype(F32)).reshape(4, 48, C)
-        x_own[i] = total
-        x_send[i] = total.astype(BF)
-        for step in (2, 1, 3):
-            x_copy(i, step).start()
-
-    def end_x(i):
+        j = i // 2
+        if i % 2 == 0:
+            x_own[j] = total
+            x_send[j] = total.astype(BF)
+            for copy in x_copies(i, x_send.at[j], x_recv.at[j]):
+                copy.start()
+        else:
+            for block in range(4):
+                for m, value in enumerate(segments(i, total[block])):
+                    y_send[j, m, block] = value.astype(BF)
+            start_y(i, y_send.at[j], y_recv.at[j])
+
+    def start_second(i):
+        j = i // 2
+        if i % 2 == 0:
+            for copy in x_copies(i, x_send.at[j], x_recv.at[j]):
+                copy.wait()
+            total = x_own[j, xi]
+            for step in (1, 2, 3):
+                total = total + x_recv[j, step - 1].astype(F32)
+            for m, value in enumerate(segments(i, total)):
+                y_send2[j, m] = value.astype(BF)
+            start_y(4 + j, y_send2.at[j], y_recv2.at[j])
+        else:
+            total = end_y(i, y_send.at[j], y_recv.at[j])
+            x_own2[j] = total
+            x_send2[j] = total.astype(BF)
+            for copy in x_copies(4 + j, x_send2.at[j], x_recv2.at[j]):
+                copy.start()
+
+    def z_copy(j, step):
+        return pltpu.make_async_remote_copy(
+            src_ref=z_send.at[j, (z + step) % 16], dst_ref=z_recv.at[j, step - 1],
+            send_sem=z_ssem.at[j, step - 1], recv_sem=z_rsem.at[j, step - 1],
+            device_id=z_id(step),
+        )
+
+    z_steps = sorted(range(1, 16), key=lambda step: -min(step, 16 - step))
+
+    def start_z(j):
+        first = end_y(4 + j, y_send2.at[j], y_recv2.at[j])
+        for copy in x_copies(4 + j, x_send2.at[j], x_recv2.at[j]):
+            copy.wait()
+        second = x_own2[j, xi]
         for step in (1, 2, 3):
-            x_copy(i, step).wait()
-        total = x_own[i, xi]
-        for step in (1, 2, 3):
-            total = total + x_recv[i, step - 1].astype(F32)
-        return total
+            second = second + x_recv2[j, step - 1].astype(F32)
+        for t in range(3):
+            lanes = slice(128 * t, 128 * t + 128)
+            z_line[j, pl.ds(t, 16, stride=8), :] = first[:, lanes]
+            z_line[j, pl.ds(t + 3, 16, stride=8), :] = second[:, lanes]
+        for t in (6, 7):
+            z_line[j, pl.ds(t, 16, stride=8), :] = jnp.zeros((16, 128), F32)
+        z_send[j] = z_line[j].reshape(16, 8, 128).astype(BF)
+        for step in z_steps:
+            z_copy(j, step).start()
+
+    def end_z(j):
+        total = z_send[j, z].astype(F32)
+        for step in z_steps[::-1]:
+            z_copy(j, step).wait()
+            total = total + z_recv[j, step - 1].astype(F32)
+        share_ref[8 * j : 8 * j + 8] = total
 
     scores_back(2, 3)
     exchange(2, west_id).wait()
@@ -471,17 +589,20 @@
     start_core(0, mm(left_o[...], branch_grad[...]))
     values_back(0, 1, 2, 3)
     start_core(1, mm(left_r[...], proj_grad[:, 2 * C : 3 * C]))
-    start_x(0)
+    start_first(0)
     scores_back(0, 1)
-    start_x(1)
+    start_first(1)
     start_core(2, mm(left_r[...], proj_grad[:, 0:C]))
     start_core(3, mm(left_r[...], proj_grad[:, C : 2 * C]))
     east_grad = mm_t(proj_grad[192:256], w_attend[...])
     east_grad = normalize_back(normed_east[...], std_east[...], east_grad)
     ex_send[3] = east_grad.astype(BF)
     exchange(3, east_id).start()
-    start_x(2)
-    start_x(3)
+    start_first(2)
+    start_first(3)
+    if scatter:
+        start_second(0)
+        start_second(1)
     copies["to_window_t"].wait()
     own_proj = mm(to_window_t[:, 0:192], proj_grad[0:192]).astype(BF)
     own_grad = mm_t(own_proj, w_attend[...])
@@ -495,97 +616,18 @@
         for row in range(14):
             grad_ref[row] = grad[row, 0:14].astype(BF)
 
-    if not scatter:
+    if scatter:
+        start_z(0)
+        start_second(2)
+        start_second(3)
+        end_features()
+        start_z(1)
+        end_z(0)
+        end_z(1)
+    else:
         end_features()
         share_ref[...] = jnp.zeros_like(share_ref)
         local_ref[...] = g_own[...]
-        return
-
-    output_sum, values_sum = end_x(0), end_x(1)
-    queries_sum, keys_sum = end_x(2), end_x(3)
-    joined = jnp.concatenate([queries_sum, keys_sum, values_sum], 1)
-    quarters = [
-        joined[:, 0:384],
-        pltpu.roll(joined[:, 256:768], 512 - 32, 1)[:, 0:384],
-        pltpu.roll(joined[:, 512:1024], 512 - 64, 1)[:, 0:384],
-        pltpu.roll(joined[:, 768:1152], 384 - 96, 1),
-    ]
-    pieces = [
-        output_sum[:, 0:128],
-        pltpu.roll(output_sum[:, 0:256], 256 - 96, 1)[:, 0:128],
-        pltpu.roll(output_sum[:, 128:384], 256 - 64, 1)[:, 0:128],
-        pltpu.roll(output_sum[:, 256:384], 128 - 32, 1),
-    ]
-    for m in range(4):
-        for i in range(3):
-            k, t = divmod(3 * m + i, 4)
-            rows = slice(16 * k, 16 * k + 16)
-            y_send[m, :, 384 * i : 384 * i + 384] = quarters[t][rows].astype(BF)
-            lanes = slice(1152 + 128 * i, 1280 + 128 * i)
-            y_send[m, :, lanes] = pieces[t][rows].astype(BF)
-
-    def y_copy(m):
-        return pltpu.make_async_remote_copy(
-            src_ref=y_send.at[m], dst_ref=y_recv.at[y], send_sem=y_ssem.at[m],
-            recv_sem=y_rsem.at[y],
-            device_id={"frame_1": 2 * core + m // 2, "frame_2": m % 2},
-        )
-
-    def y_landed(source):
-        return pltpu.make_async_remote_copy(
-            src_ref=y_send.at[0], dst_ref=y_recv.at[source], send_sem=y_ssem.at[0],
-            recv_sem=y_rsem.at[source], device_id={"frame_2": 1 - core},
-        )
-
-    for m in range(4):
-        mine = jnp.logical_and(2 * core + m // 2 == y, core == m % 2)
-
-        @pl.when(mine)
-        def _():
-            y_recv[y] = y_send[m]
-
-        @pl.when(jnp.logical_not(mine))
-        def _():
-            y_copy(m).start()
-
-    for source in range(4):
-        mine = jnp.logical_and(y == source, y // 2 == core)
-
-        @pl.when(jnp.logical_not(mine))
-        def _():
-            y_landed(source).wait_recv()
-
-    total = y_recv[0].astype(F32)
-    for source in range(1, 4):
-        total = total + y_recv[source].astype(F32)
-    for t in range(12):
-        z_line[pl.ds(t, 16, stride=16), :] = total[:, 128 * t : 128 * t + 128]
-    for t in range(12, 16):
-        z_line[pl.ds(t, 16, stride=16), :] = jnp.zeros((16, 128), F32)
-    z_send[...] = z_line[...].reshape(16, 16, 128).astype(BF)
-
-    def z_copy(step):
-        return pltpu.make_async_remote_copy(
-            src_ref=z_send.at[(z + step) % 16], dst_ref=z_recv.at[step - 1],
-            send_sem=z_ssem.at[step - 1], recv_sem=z_rsem.at[step - 1], device_id=z_id(step),
-        )
-
-    steps = sorted(range(1, 16), key=lambda step: -min(step, 16 - step))
-    for step in steps:
-        z_copy(step).start()
-    end_features()
-    for m in range(4):
-        mine = jnp.logical_and(2 * core + m // 2 == y, core == m % 2)
-
-        @pl.when(jnp.logical_not(mine))
-        def _():
-            y_copy(m).wait_send()
-
-    total = z_send[z].astype(F32)
-    for step in steps[::-1]:
-        z_copy(step).wait()
-        total = total + z_recv[step - 1].astype(F32)
-    share_ref[...] = total
 
 
 def finish(merged_in, grad_in, share, merged_ref, grad_ref, attend_ref, output_ref):
@@ -593,28 +635,36 @@
     grad_ref[0] = grad_in[...]
     lane = lax.broadcasted_iota(jnp.int32, (1, 128), 1)
 
-    def row(i, turn=0):
-        value = share[i : i + 1, :]
-        return pltpu.roll(value, turn, 1) if turn else value
-
-    one = [row(i, 32) for i in (3, 4, 5)]
-    two = [row(i, 64) for i in (6, 7, 8)]
-    low, half = lane < 32, lane < 64
-    attend = [
-        row(0),
-        row(1),
-        jnp.where(low, row(2), one[0]),
-        jnp.where(low, one[0], one[1]),
-        jnp.where(low, one[1], jnp.where(half, one[2], two[0])),
-        jnp.where(half, two[0], two[1]),
-        jnp.where(half, two[1], two[2]),
-    ]
-    middle, last = row(10, 96), row(11, 64)
-    output = [jnp.where(lane < 96, row(9), middle), jnp.where(half, middle, last), last]
-    for ref, rows in ((attend_ref, attend), (output_ref, output)):
-        for i, value in enumerate(rows):
-            count = min(128, ref.shape[0] - 128 * i)
-            ref[128 * i : 128 * i + count] = value.reshape(128)[:count]
+    def put(ref, pieces):
+        lines = [jnp.zeros((1, 128), F32) for _ in range(-(-ref.shape[0] // 128))]
+        start = 0
+        for first, width in pieces:
+            skip, turn = divmod(start, 128)
+            values = [share[first + i : first + i + 1, :] for i in range(3)]
+            if turn:
+                values = [pltpu.roll(value, turn, 1) for value in values]
+            for j in range(skip, (start + width - 1) // 128 + 1):
+                value = values[min(j - skip, 2)]
+                if turn and j > skip:
+                    value = jnp.where(lane < turn, values[j - skip - 1], value)
+                at = lane + 128 * j
+                inside = jnp.logical_and(at >= start, at < start + width)
+                lines[j] = jnp.where(inside, value, lines[j])
+            start += width
+        for j, value in enumerate(lines):
+            count = min(128, ref.shape[0] - 128 * j)
+            ref[128 * j : 128 * j + count] = value.reshape(128)[:count]
+
+    put(output_ref, ((0, 288),))
+    v, q, k = 3, 8, 11
+    segment = 2 * (lax.axis_index("frame_1") % 2) + lax.axis_index("frame_2")
+    for m, pieces in enumerate((
+        ((q, 384), (k, 384), (v, 96)),
+        ((v, 288), (q, 384), (k, 192)),
+        ((k, 192), (v, 384), (q, 288)),
+        ((q, 96), (k, 384), (v, 384)),
+    )):
+        pl.when(segment == m)(functools.partial(put, attend_ref, pieces))
 
 
 def local_call(scatter, features, position_bias, attend_weight, output_weight, merge_weight, cotangent):
@@ -647,16 +697,21 @@
         pltpu.VMEM((4, 2, 192, C), F32),
         pltpu.VMEM((4, 2, 192, C), BF),
         pltpu.VMEM((4, 192, C), BF),
-        pltpu.VMEM((4, 4, 48, C), F32),
-        pltpu.VMEM((4, 4, 48, C), BF),
-        pltpu.VMEM((4, 3, 48, C), BF),
-        pltpu.VMEM((4, 16, 1536), BF),
-        pltpu.VMEM((4, 16, 1536), BF),
-        pltpu.VMEM((256, 128), F32),
-        pltpu.VMEM((16, 16, 128), BF),
-        pltpu.VMEM((15, 16, 128), BF),
-        dma((N_IN,)), dma((4,)), dma((4,)), dma((4,)), dma((4,)), dma((4, 3)), dma((4, 3)),
-        dma((4,)), dma((4,)), dma((15,)), dma((15,)), pltpu.SemaphoreType.REGULAR((3,)),
+        pltpu.VMEM((2, 4, 48, C), F32),
+        pltpu.VMEM((2, 4, 48, C), BF),
+        pltpu.VMEM((2, 3, 48, C), BF),
+        pltpu.VMEM((2, 4, 4, 16, C), BF),
+        pltpu.VMEM((2, 4, 4, 16, C), BF),
+        pltpu.VMEM((2, 4, 16, C), F32),
+        pltpu.VMEM((2, 4, 16, C), BF),
+        pltpu.VMEM((2, 3, 16, C), BF),
+        pltpu.VMEM((2, 4, 16, C), BF),
+        pltpu.VMEM((2, 4, 16, C), BF),
+        pltpu.VMEM((2, 128, 128), F32),
+        pltpu.VMEM((2, 16, 8, 128), BF),
+        pltpu.VMEM((2, 15, 8, 128), BF),
+        dma((N_IN,)), dma((4,)), dma((4,)), dma((4,)), dma((4,)), dma((6, 3)), dma((6, 3)),
+        dma((6, 4)), dma((6, 4)), dma((2, 15)), dma((2, 15)), pltpu.SemaphoreType.REGULAR((3,)),
     ]
     vmem = pl.BlockSpec(memory_space=pltpu.VMEM)
     return pl.pallas_call(

time: 54.9 us -> 53.9 us (0.982)
  Pallas kernels: 54 us -> 53.1 us
    pallas_call x1, Pallas kernels: 52.3 us -> 51.3 us  [local_call(): pl.pallas_call(functools.partial(kernel, scatter), out_shape=(jax.ShapeDt...]
where the time goes in v1:
time: 53.9 us; the launch traced here: 53.7 us
  Pallas kernels  53.1 us (99%)
  between operations  0.64 us (1%)
    pallas_call x1, Pallas kernels, local_call(): pl.pallas_call(functools.partial(kernel, scatter), out_shape=(jax.ShapeDt...  51.3 us
    pallas_call x1, Pallas kernels, per_device(): pl.pallas_call(finish, out_shape=(jax.ShapeDtypeStruct((1, *merged.shape)...  1.78 us

profile of v1, /device:TPU:1, one launch (start us, length us, event | category | flops | bytes accessed | tf_op | source)
XLA Modules:
  0.0 53.7 jit_solution(8713494230922677359)
XLA Ops:
  0.6 51.3 %shard_map.174 = (bf16[7,7,768]{2,1,0:T(8,128)(2,1)}, bf16[14,14,384]{2,1,0:T(8,128)(2,1)}, f32[16,128]{1,0:T(8,128)}) custom-call(bf16[14,14,384]{2,1,0:T(8,128)(2,1)} %bitcast.3, bf16[7,7,768]{2,1,0:T(8,128)(2,1)} %bitcast.4, f32[12,169]{1,0:T(8,128)} %bitcast.5, bf16[384,1152]{1,0:T(8,128)(2,1)} %refs_3_.1, bf16[384,384]{1,0:T(8,128)(2,1)} %refs_4_.1, ...), custom_call_target="tpu_custom_call" | custom-call | tf_op jit(solution)/shard_map/pallas_call | solution.py:717
  52.0 1.8 %shard_map.175 = (bf16[1,7,7,768]{3,2,1,0:T(8,128)(2,1)}, bf16[1,14,14,384]{3,2,1,0:T(8,128)(2,1)}, f32[864]{0:T(1024)}, f32[288]{0:T(512)}) custom-call(bf16[7,7,768]{2,1,0:T(8,128)(2,1)} %get-tuple-element.7.merged_in, bf16[14,14,384]{2,1,0:T(8,128)(2,1)} %get-tuple-element.8.grad_in, f32[16,128]{1,0:T(8,128)} %get-tuple-element.9.share), custom_call_target="tpu_custom_call" | custom-call | tf_op jit(solution)/shard_map/pallas_call | solution.py:735

commit v2 on v1

--- a/solution.py
+++ b/solution.py
@@ -600,9 +600,6 @@
     exchange(3, east_id).start()
     start_first(2)
     start_first(3)
-    if scatter:
-        start_second(0)
-        start_second(1)
     copies["to_window_t"].wait()
     own_proj = mm(to_window_t[:, 0:192], proj_grad[0:192]).astype(BF)
     own_grad = mm_t(own_proj, w_attend[...])
@@ -617,11 +614,11 @@
             grad_ref[row] = grad[row, 0:14].astype(BF)
 
     if scatter:
+        for group in range(4):
+            start_second(group)
         start_z(0)
-        start_second(2)
-        start_second(3)
+        start_z(1)
         end_features()
-        start_z(1)
         end_z(0)
         end_z(1)
     else:
@@ -717,9 +714,9 @@
     return pl.pallas_call(
         functools.partial(kernel, scatter),
         out_shape=(
-            jax.ShapeDtypeStruct((7, 7, OUT), BF),
-            jax.ShapeDtypeStruct((14, 14, C), BF),
-            jax.ShapeDtypeStruct((16, 128), F32),
+            pltpu.VMEM((7, 7, OUT), BF),
+            pltpu.VMEM((14, 14, C), BF),
+            pltpu.VMEM((16, 128), F32),
         )
         + (() if scatter else (jax.ShapeDtypeStruct((4, 2, 192, C), F32),)),
         in_specs=[pl.BlockSpec(memory_space=pl.ANY)] * N_IN,
@@ -742,6 +739,7 @@
         ),
         in_specs=(vmem,) * 3,
         out_specs=(vmem,) * 4,
+        compiler_params=pltpu.CompilerParams(vmem_limit_bytes=8 << 20),
     )(merged, feature_grad, share)
 
 

time: 53.9 us -> 50.5 us (0.937)
  Pallas kernels: 53.1 us -> 49.7 us
    pallas_call x1, Pallas kernels: 51.3 us -> 48.9 us  [local_call(): pl.pallas_call(functools.partial(kernel, scatter), out_shape=(pltpu.VMEM(...]
    pallas_call x1, Pallas kernels: 1.78 us -> 0.81 us  [per_device(): pl.pallas_call(finish, out_shape=(jax.ShapeDtypeStruct((1, *merged.shape)...]
where the time goes in v2:
time: 50.5 us; the launch traced here: 50.4 us
  Pallas kernels  49.7 us (98%)
  between operations  0.64 us (1%)
    pallas_call x1, Pallas kernels, local_call(): pl.pallas_call(functools.partial(kernel, scatter), out_shape=(pltpu.VMEM(...  48.9 us

profile of v2, /device:TPU:1, one launch (start us, length us, event | category | flops | bytes accessed | tf_op | source)
XLA Modules:
  0.0 50.4 jit_solution(13235083841415442478)
XLA Ops:
  0.6 48.9 %shard_map.174 = (bf16[7,7,768]{2,1,0:T(8,128)(2,1)S(1)}, bf16[14,14,384]{2,1,0:T(8,128)(2,1)S(1)}, f32[16,128]{1,0:T(8,128)S(1)}) custom-call(bf16[14,14,384]{2,1,0:T(8,128)(2,1)} %bitcast.3, bf16[7,7,768]{2,1,0:T(8,128)(2,1)} %bitcast.4, f32[12,169]{1,0:T(8,128)} %bitcast.5, bf16[384,1152]{1,0:T(8,128)(2,1)} %refs_3_.1, bf16[384,384]{1,0:T(8,128)(2,1)} %refs_4_.1, ...), custom_call_target="tpu_custom_call" | custom-call | tf_op jit(solution)/shard_map/pallas_call | solution.py:714
  49.6 0.8 %shard_map.175 = (bf16[1,7,7,768]{3,2,1,0:T(8,128)(2,1)}, bf16[1,14,14,384]{3,2,1,0:T(8,128)(2,1)}, f32[864]{0:T(1024)}, f32[288]{0:T(512)}) custom-call(bf16[7,7,768]{2,1,0:T(8,128)(2,1)S(1)} %get-tuple-element.7.merged_in, bf16[14,14,384]{2,1,0:T(8,128)(2,1)S(1)} %get-tuple-element.8.grad_in, f32[16,128]{1,0:T(8,128)S(1)} %get-tuple-element.9.share), custom_call_target="tpu_custom_call" | custom-call | tf_op jit(solution)/shard_map/pallas_call | solution.py:732

commit v3 on v2

--- a/solution.py
+++ b/solution.py
@@ -165,7 +165,7 @@
     (
         x_scr, cot_scr, table_scr, bias_a, bias_b, normed_scr, std_scr,
         normed_east, std_east, qkv, probs, attended, branch_grad, outer, proj_grad,
-        hidden_grad, left_o, left_r, feature_scr,
+        hidden_grad, left_o, left_r, feature_scr, first_scr,
         ex_send, ex_recv,
         g_own, g_send, g_recv, x_own, x_send, x_recv, y_send, y_recv,
         x_own2, x_send2, x_recv2, y_send2, y_recv2, z_line, z_send, z_recv,
@@ -180,7 +180,7 @@
         name: pltpu.make_async_copy(given[i], held[i], in_sem.at[i])
         for i, name in enumerate(NAMES)
     }
-    for name in ORDER:
+    for name in ORDER[:2]:
         copies[name].start()
 
     z, x_lo = lax.axis_index("azim_0"), lax.axis_index("azim_1")
@@ -217,16 +217,23 @@
             recv_sem=ex_rsem.at[i], device_id=device,
         )
 
+    for name in ORDER[2:7]:
+        copies[name].start()
     copies["feat"].wait()
+    for name in ORDER[7:]:
+        copies[name].start()
     x_scr[...] = jnp.zeros_like(x_scr)
     for row in range(14):
         x_scr[row, 0:14, :] = feat[row].astype(F32)
     tokens = x_scr[...].reshape(224, C)
     tokens16 = tokens.astype(BF)
     copies["to_window"].wait()
-    ex_send[0] = mm(to_window[192:256], tokens16).astype(BF)
+    shared = mm(to_window[128:256], tokens16).astype(BF)
+    ex_send[0] = shared[64:128]
+    ex_send[1] = shared[0:64]
     pl.semaphore_wait(barrier, len(near))
     exchange(0, west_id).start()
+    exchange(1, east_id).start()
     if scatter:
         for step in (1, -1):
             pl.semaphore_signal(near_sem.at[0], inc=1, device_id=z_id(step))
@@ -242,9 +249,12 @@
     normed, inverse_std = normalize(tokens)
     normed_scr[...] = normed
     std_scr[...] = inverse_std
-    rolled_own = mm(to_window[0:192], normed.astype(BF)).astype(BF)
+    rolled = mm(to_window[...], normed.astype(BF)).astype(BF)
+    rolled_own = rolled[0:192]
     copies["w_attend"].wait()
-    qkv[0:192] = mm(rolled_own, w_attend[...]).astype(BF)
+    projected = mm(rolled, w_attend[...]).astype(BF)
+    qkv[0:192] = projected[0:192]
+    qkv[320:384] = projected[192:256]
 
     copies["pos"].wait()
     copies["index"].wait()
@@ -284,14 +294,6 @@
     copies["w_merge"].wait()
     quad_grad_in = mm_t(cot_scr[...].reshape(64, OUT).astype(BF), w_merge[...])
 
-    exchange(0, west_id).wait()
-    widen_reach(0)
-    normed, inverse_std = normalize(ex_recv[0].astype(F32))
-    normed_east[...] = normed
-    std_east[...] = inverse_std
-    rolled_east = normed.astype(BF)
-    qkv[192:256] = mm(rolled_east, w_attend[...]).astype(BF)
-
     head_lanes = [(lane // 32 == h).astype(F32).astype(BF) for h in range(4)]
 
     def spread(block):
@@ -317,11 +319,12 @@
     ones = ones.astype(F32).astype(BF)
 
     def half_sums(values):
+        rows = values[0].shape[0]
         joined = jnp.concatenate(values, 0)
         high = joined.astype(BF)
         rest = (joined - high.astype(F32)).astype(BF)
         total = mm(high, ones) + mm(rest, ones)
-        return [total[64 * i : 64 * i + 64] for i in range(len(values))]
+        return [total[rows * i : rows * i + rows] for i in range(len(values))]
 
     def split_halves(wide):
         return [part[:, 128 * i : 128 * i + 128] for part in wide for i in range(2)]
@@ -332,20 +335,23 @@
             for i in range(0, len(parts), 2)
         ]
 
+    def softmax(units, scores, rows):
+        parts = split_halves(scores)
+        for i, (a, g) in enumerate(units):
+            for j in range(2):
+                bias = pair_bias(2 * g + j)[rows] + mask[a, rows]
+                parts[2 * i + j] = parts[2 * i + j] * SCALE + bias
+        tops = [halves(jnp.max, -3e38, low, part) for part in parts]
+        parts = [jnp.exp(part - top) for part, top in zip(parts, tops)]
+        sums = half_sums(parts)
+        return [part * (1.0 / total) for part, total in zip(parts, sums)]
+
     def attend(*windows):
         units = units_of(windows)
         scores = [
             mm_t(of_window(qkv, w, 0, g), spread(of_window(qkv, w, 1, g))) for w, g in units
         ]
-        parts = split_halves(scores)
-        for i, (w, g) in enumerate(units):
-            for j in range(2):
-                bias = pair_bias(2 * g + j) + mask[WINDOWS[w][0]]
-                parts[2 * i + j] = parts[2 * i + j] * SCALE + bias
-        tops = [halves(jnp.max, -3e38, low, part) for part in parts]
-        parts = [jnp.exp(part - top) for part, top in zip(parts, tops)]
-        sums = half_sums(parts)
-        parts = [part * (1.0 / total) for part, total in zip(parts, sums)]
+        parts = softmax([(WINDOWS[w][0], g) for w, g in units], scores, slice(0, 64))
         for i, (w, g) in enumerate(units):
             for j in range(2):
                 probs[GROUPS * w + g, :, 128 * j : 128 * j + 128] = parts[2 * i + j]
@@ -353,22 +359,43 @@
             result = mm(prob, spread(of_window(qkv, w, 2, g))).astype(BF)
             put_window(attended, *WINDOWS[w], group_lanes(0, g), result)
 
+    def attend_first():
+        units = [(a, g) for a in range(2) for g in range(GROUPS)]
+
+        def part(a, kind, g):
+            lanes = group_lanes(kind, g)
+            near, far = 256 + 32 * a, 320 + 32 * a
+            return jnp.concatenate([qkv[near : near + 32, lanes], qkv[far : far + 32, lanes]], 0)
+
+        scores = [
+            mm_t(qkv[320 + 32 * a : 352 + 32 * a, group_lanes(0, g)], spread(part(a, 1, g)))
+            for a, g in units
+        ]
+        parts = softmax(units, scores, slice(32, 64))
+        for (a, g), prob in zip(units, join_halves(parts)):
+            result = mm(prob, spread(part(a, 2, g))).astype(BF)
+            first_scr[32 * a : 32 * a + 32, group_lanes(0, g)] = result
+
+    attend(2, 3)
+
+    exchange(0, west_id).wait()
+    exchange(1, east_id).wait()
+    widen_reach(0)
+    normed, inverse_std = normalize(ex_recv[0:2].astype(F32).reshape(128, C))
+    normed_east[...] = normed[0:64]
+    std_east[...] = inverse_std[0:64]
+    rolled = normed.astype(BF)
+    rolled_east = rolled[0:64]
+    qkv[192:320] = mm(rolled, w_attend[...]).astype(BF)
+    attend_first()
     attend(0, 1)
-    ex_send[1] = attended[192:256]
-    exchange(1, east_id).start()
-    attend(2, 3)
-    copies["row_pick"].wait()
-    left_r[:, 0:192] = mm_t(row_pick[...], rolled_own).astype(BF)
-    left_r[:, 192:256] = mm_t(row_pick[...], rolled_east).astype(BF)
-    left_o[...] = mm_t(row_pick[...], attended[...]).astype(BF)
     copies["to_quad"].wait()
     copies["win_quad"].wait()
     copies["w_out"].wait()
     features_quad = mm(to_quad[...], tokens16)
-    exchange(1, east_id).wait()
     widen_reach(1)
 
-    extended = jnp.concatenate([attended[0:192], ex_recv[1]], 0)
+    extended = jnp.concatenate([attended[0:192], first_scr[...]], 0)
     attended_quad = mm(win_quad[...], extended).astype(BF)
     hidden = (features_quad + mm(attended_quad, w_out[...])).astype(BF).astype(F32)
     quads = [hidden[64 * e : 64 * e + 64] for e in range(4)]
@@ -390,6 +417,10 @@
     copies["win_quad_t"].wait()
     ex_send[2] = mm(win_quad_t[192:256], hidden_grad[...]).astype(BF)
     exchange(2, west_id).start()
+    copies["row_pick"].wait()
+    left_r[:, 0:192] = mm_t(row_pick[...], rolled_own).astype(BF)
+    left_r[:, 192:256] = mm_t(row_pick[...], rolled_east).astype(BF)
+    left_o[...] = mm_t(row_pick[...], attended[...]).astype(BF)
     own_grad = mm(win_quad_t[0:192], hidden_grad[...]).astype(BF)
     branch_grad[0:192] = own_grad
     outer[0:192] = mm_t(own_grad, w_out[...]).astype(BF)
@@ -679,7 +710,7 @@
         pltpu.VMEM((224, 1), F32),
         pltpu.VMEM((64, C), F32),
         pltpu.VMEM((64, 1), F32),
-        pltpu.VMEM((256, 3 * C), BF),
+        pltpu.VMEM((384, 3 * C), BF),
         pltpu.VMEM((12, 64, 256), F32),
         pltpu.VMEM((256, C), BF),
         pltpu.VMEM((256, C), BF),
@@ -689,6 +720,7 @@
         pltpu.VMEM((C, 256), BF),
         pltpu.VMEM((C, 256), BF),
         pltpu.VMEM((224, C), F32),
+        pltpu.VMEM((64, C), BF),
         pltpu.VMEM((4, 64, C), BF),
         pltpu.VMEM((4, 64, C), BF),
         pltpu.VMEM((4, 2, 192, C), F32),

time: 50.5 us -> 47 us (0.931)
  Pallas kernels: 49.7 us -> 46.2 us
    pallas_call x1, Pallas kernels: 48.9 us -> 45.4 us  [local_call(): pl.pallas_call(functools.partial(kernel, scatter), out_shape=(pltpu.VMEM(...]
where the time goes in v3:
time: 47 us; the launch traced here: 46.9 us
  Pallas kernels  46.2 us (98%)
  between operations  0.64 us (1%)
    pallas_call x1, Pallas kernels, local_call(): pl.pallas_call(functools.partial(kernel, scatter), out_shape=(pltpu.VMEM(...  45.4 us

profile of v3, /device:TPU:1, one launch (start us, length us, event | category | flops | bytes accessed | tf_op | source)
XLA Modules:
  0.0 46.9 jit_solution(9621029363500420943)
XLA Ops:
  0.6 45.4 %shard_map.174 = (bf16[7,7,768]{2,1,0:T(8,128)(2,1)S(1)}, bf16[14,14,384]{2,1,0:T(8,128)(2,1)S(1)}, f32[16,128]{1,0:T(8,128)S(1)}) custom-call(bf16[14,14,384]{2,1,0:T(8,128)(2,1)} %bitcast.3, bf16[7,7,768]{2,1,0:T(8,128)(2,1)} %bitcast.4, f32[12,169]{1,0:T(8,128)} %bitcast.5, bf16[384,1152]{1,0:T(8,128)(2,1)} %refs_3_.1, bf16[384,384]{1,0:T(8,128)(2,1)} %refs_4_.1, ...), custom_call_target="tpu_custom_call" | custom-call | tf_op jit(solution)/shard_map/pallas_call | solution.py:746
  46.1 0.8 %shard_map.175 = (bf16[1,7,7,768]{3,2,1,0:T(8,128)(2,1)}, bf16[1,14,14,384]{3,2,1,0:T(8,128)(2,1)}, f32[864]{0:T(1024)}, f32[288]{0:T(512)}) custom-call(bf16[7,7,768]{2,1,0:T(8,128)(2,1)S(1)} %get-tuple-element.7.merged_in, bf16[14,14,384]{2,1,0:T(8,128)(2,1)S(1)} %get-tuple-element.8.grad_in, f32[16,128]{1,0:T(8,128)S(1)} %get-tuple-element.9.share), custom_call_target="tpu_custom_call" | custom-call | tf_op jit(solution)/shard_map/pallas_call | solution.py:764

commit v4 on v3

--- a/solution.py
+++ b/solution.py
@@ -319,12 +319,12 @@
     ones = ones.astype(F32).astype(BF)
 
     def half_sums(values):
-        rows = values[0].shape[0]
         joined = jnp.concatenate(values, 0)
         high = joined.astype(BF)
         rest = (joined - high.astype(F32)).astype(BF)
         total = mm(high, ones) + mm(rest, ones)
-        return [total[rows * i : rows * i + rows] for i in range(len(values))]
+        ends = [sum(value.shape[0] for value in values[: i + 1]) for i in range(len(values))]
+        return [total[end - value.shape[0] : end] for value, end in zip(values, ends)]
 
     def split_halves(wide):
         return [part[:, 128 * i : 128 * i + 128] for part in wide for i in range(2)]
@@ -335,9 +335,9 @@
             for i in range(0, len(parts), 2)
         ]
 
-    def softmax(units, scores, rows):
+    def softmax(units, scores):
         parts = split_halves(scores)
-        for i, (a, g) in enumerate(units):
+        for i, (a, g, rows) in enumerate(units):
             for j in range(2):
                 bias = pair_bias(2 * g + j)[rows] + mask[a, rows]
                 parts[2 * i + j] = parts[2 * i + j] * SCALE + bias
@@ -346,37 +346,39 @@
         sums = half_sums(parts)
         return [part * (1.0 / total) for part, total in zip(parts, sums)]
 
-    def attend(*windows):
+    def of_first(a, kind, g):
+        lanes = group_lanes(kind, g)
+        near, far = 256 + 32 * a, 320 + 32 * a
+        return jnp.concatenate([qkv[near : near + 32, lanes], qkv[far : far + 32, lanes]], 0)
+
+    def attend(*windows, first=()):
         units = units_of(windows)
+        extra = [(a, g) for a in first for g in range(GROUPS)]
         scores = [
             mm_t(of_window(qkv, w, 0, g), spread(of_window(qkv, w, 1, g))) for w, g in units
+        ] + [
+            mm_t(qkv[320 + 32 * a : 352 + 32 * a, group_lanes(0, g)], spread(of_first(a, 1, g)))
+            for a, g in extra
         ]
-        parts = softmax([(WINDOWS[w][0], g) for w, g in units], scores, slice(0, 64))
+        parts = softmax(
+            [(WINDOWS[w][0], g, slice(0, 64)) for w, g in units]
+            + [(a, g, slice(32, 64)) for a, g in extra],
+            scores,
+        )
         for i, (w, g) in enumerate(units):
             for j in range(2):
                 probs[GROUPS * w + g, :, 128 * j : 128 * j + 128] = parts[2 * i + j]
-        for (w, g), prob in zip(units, join_halves(parts)):
+        joined = join_halves(parts)
+        for (w, g), prob in zip(units, joined):
             result = mm(prob, spread(of_window(qkv, w, 2, g))).astype(BF)
             put_window(attended, *WINDOWS[w], group_lanes(0, g), result)
-
-    def attend_first():
-        units = [(a, g) for a in range(2) for g in range(GROUPS)]
-
-        def part(a, kind, g):
-            lanes = group_lanes(kind, g)
-            near, far = 256 + 32 * a, 320 + 32 * a
-            return jnp.concatenate([qkv[near : near + 32, lanes], qkv[far : far + 32, lanes]], 0)
-
-        scores = [
-            mm_t(qkv[320 + 32 * a : 352 + 32 * a, group_lanes(0, g)], spread(part(a, 1, g)))
-            for a, g in units
-        ]
-        parts = softmax(units, scores, slice(32, 64))
-        for (a, g), prob in zip(units, join_halves(parts)):
-            result = mm(prob, spread(part(a, 2, g))).astype(BF)
+        for (a, g), prob in zip(extra, joined[len(units) :]):
+            result = mm(prob, spread(of_first(a, 2, g))).astype(BF)
             first_scr[32 * a : 32 * a + 32, group_lanes(0, g)] = result
 
     attend(2, 3)
+    copies["to_quad"].wait()
+    features_quad = mm(to_quad[...], tokens16)
 
     exchange(0, west_id).wait()
     exchange(1, east_id).wait()
@@ -387,12 +389,9 @@
     rolled = normed.astype(BF)
     rolled_east = rolled[0:64]
     qkv[192:320] = mm(rolled, w_attend[...]).astype(BF)
-    attend_first()
-    attend(0, 1)
-    copies["to_quad"].wait()
+    attend(0, 1, first=(0, 1))
     copies["win_quad"].wait()
     copies["w_out"].wait()
-    features_quad = mm(to_quad[...], tokens16)
     widen_reach(1)
 
     extended = jnp.concatenate([attended[0:192], first_scr[...]], 0)

time: 47 us -> 47 us (level)
  no operation moved by 1% of the time
where the time goes in v4:
time: 47 us; the launch traced here: 46.9 us
  Pallas kernels  46.2 us (98%)
  between operations  0.64 us (1%)
    pallas_call x1, Pallas kernels, local_call(): pl.pallas_call(functools.partial(kernel, scatter), out_shape=(pltpu.VMEM(...  45.4 us

profile of v4, /device:TPU:1, one launch (start us, length us, event | category | flops | bytes accessed | tf_op | source)
XLA Modules:
  0.0 46.9 jit_solution(10332678995922359083)
XLA Ops:
  0.6 45.4 %shard_map.174 = (bf16[7,7,768]{2,1,0:T(8,128)(2,1)S(1)}, bf16[14,14,384]{2,1,0:T(8,128)(2,1)S(1)}, f32[16,128]{1,0:T(8,128)S(1)}) custom-call(bf16[14,14,384]{2,1,0:T(8,128)(2,1)} %bitcast.3, bf16[7,7,768]{2,1,0:T(8,128)(2,1)} %bitcast.4, f32[12,169]{1,0:T(8,128)} %bitcast.5, bf16[384,1152]{1,0:T(8,128)(2,1)} %refs_3_.1, bf16[384,384]{1,0:T(8,128)(2,1)} %refs_4_.1, ...), custom_call_target="tpu_custom_call" | custom-call | tf_op jit(solution)/shard_map/pallas_call | solution.py:745
  46.1 0.8 %shard_map.175 = (bf16[1,7,7,768]{3,2,1,0:T(8,128)(2,1)}, bf16[1,14,14,384]{3,2,1,0:T(8,128)(2,1)}, f32[864]{0:T(1024)}, f32[288]{0:T(512)}) custom-call(bf16[7,7,768]{2,1,0:T(8,128)(2,1)S(1)} %get-tuple-element.7.merged_in, bf16[14,14,384]{2,1,0:T(8,128)(2,1)S(1)} %get-tuple-element.8.grad_in, f32[16,128]{1,0:T(8,128)S(1)} %get-tuple-element.9.share), custom_call_target="tpu_custom_call" | custom-call | tf_op jit(solution)/shard_map/pallas_call | solution.py:763

commit v5 on v3

--- a/solution.py
+++ b/solution.py
@@ -152,6 +152,8 @@
     "to_quad", "win_quad", "w_out", "win_quad_t", "to_quad_t", "to_window_t",
 )
 N_IN = len(NAMES)
+X_SLOTS = {0: 0, 2: 1, 4: 2, 5: 3}
+Y_SLOTS = {1: 0, 3: 1, 4: 2, 5: 3}
 
 
 def kernel(scatter, *refs):
@@ -474,23 +476,32 @@
         return [
             pltpu.make_async_remote_copy(
                 src_ref=sent.at[(xi + step) % 4], dst_ref=landing.at[step - 1],
-                send_sem=x_ssem.at[i, step - 1], recv_sem=x_rsem.at[i, step - 1],
+                send_sem=x_ssem.at[X_SLOTS[i]], recv_sem=x_rsem.at[X_SLOTS[i]],
                 device_id=x_id(step),
             )
             for step in (2, 1, 3)
         ]
 
+    def end_all(landing, sent_sem, landed_sem):
+        pltpu.make_async_remote_copy(
+            src_ref=landing, dst_ref=landing, send_sem=sent_sem, recv_sem=landed_sem,
+            device_id={"frame_2": 1 - core},
+        ).wait()
+
+    def end_x(i, landing):
+        end_all(landing, x_ssem.at[X_SLOTS[i]], x_rsem.at[X_SLOTS[i]])
+
     def y_copy(i, m, sent, landing):
         return pltpu.make_async_remote_copy(
-            src_ref=sent.at[m], dst_ref=landing.at[y], send_sem=y_ssem.at[i, m],
-            recv_sem=y_rsem.at[i, y],
+            src_ref=sent.at[m], dst_ref=landing.at[y], send_sem=y_ssem.at[Y_SLOTS[i], m],
+            recv_sem=y_rsem.at[Y_SLOTS[i], y],
             device_id={"frame_1": 2 * core + m // 2, "frame_2": m % 2},
         )
 
     def y_landed(i, source, sent, landing):
         return pltpu.make_async_remote_copy(
-            src_ref=sent.at[0], dst_ref=landing.at[source], send_sem=y_ssem.at[i, 0],
-            recv_sem=y_rsem.at[i, source], device_id={"frame_2": 1 - core},
+            src_ref=sent.at[0], dst_ref=landing.at[source], send_sem=y_ssem.at[Y_SLOTS[i], 0],
+            recv_sem=y_rsem.at[Y_SLOTS[i], source], device_id={"frame_2": 1 - core},
         )
 
     def stays(m):
@@ -564,8 +575,7 @@
     def start_second(i):
         j = i // 2
         if i % 2 == 0:
-            for copy in x_copies(i, x_send.at[j], x_recv.at[j]):
-                copy.wait()
+            end_x(i, x_recv.at[j])
             total = x_own[j, xi]
             for step in (1, 2, 3):
                 total = total + x_recv[j, step - 1].astype(F32)
@@ -582,16 +592,14 @@
     def z_copy(j, step):
         return pltpu.make_async_remote_copy(
             src_ref=z_send.at[j, (z + step) % 16], dst_ref=z_recv.at[j, step - 1],
-            send_sem=z_ssem.at[j, step - 1], recv_sem=z_rsem.at[j, step - 1],
-            device_id=z_id(step),
+            send_sem=z_ssem.at[j], recv_sem=z_rsem.at[j], device_id=z_id(step),
         )
 
     z_steps = sorted(range(1, 16), key=lambda step: -min(step, 16 - step))
 
     def start_z(j):
         first = end_y(4 + j, y_send2.at[j], y_recv2.at[j])
-        for copy in x_copies(4 + j, x_send2.at[j], x_recv2.at[j]):
-            copy.wait()
+        end_x(4 + j, x_recv2.at[j])
         second = x_own2[j, xi]
         for step in (1, 2, 3):
             second = second + x_recv2[j, step - 1].astype(F32)
@@ -607,8 +615,8 @@
 
     def end_z(j):
         total = z_send[j, z].astype(F32)
-        for step in z_steps[::-1]:
-            z_copy(j, step).wait()
+        end_all(z_recv.at[j], z_ssem.at[j], z_rsem.at[j])
+        for step in z_steps:
             total = total + z_recv[j, step - 1].astype(F32)
         share_ref[8 * j : 8 * j + 8] = total
 
@@ -739,8 +747,8 @@
         pltpu.VMEM((2, 128, 128), F32),
         pltpu.VMEM((2, 16, 8, 128), BF),
         pltpu.VMEM((2, 15, 8, 128), BF),
-        dma((N_IN,)), dma((4,)), dma((4,)), dma((4,)), dma((4,)), dma((6, 3)), dma((6, 3)),
-        dma((6, 4)), dma((6, 4)), dma((2, 15)), dma((2, 15)), pltpu.SemaphoreType.REGULAR((3,)),
+        dma((N_IN,)), dma((4,)), dma((4,)), dma((4,)), dma((4,)), dma((4,)), dma((4,)),
+        dma((4, 4)), dma((4, 4)), dma((2,)), dma((2,)), pltpu.SemaphoreType.REGULAR((3,)),
     ]
     vmem = pl.BlockSpec(memory_space=pltpu.VMEM)
     return pl.pallas_call(

time: 47 us -> 46.1 us (0.981)
  Pallas kernels: 46.2 us -> 45.3 us
    pallas_call x1, Pallas kernels: 45.4 us -> 44.5 us  [local_call(): pl.pallas_call(functools.partial(kernel, scatter), out_shape=(pltpu.VMEM(...]
where the time goes in v5:
time: 46.1 us; the launch traced here: 46 us
  Pallas kernels  45.3 us (98%)
  between operations  0.64 us (1%)
    pallas_call x1, Pallas kernels, local_call(): pl.pallas_call(functools.partial(kernel, scatter), out_shape=(pltpu.VMEM(...  44.5 us

profile of v5, /device:TPU:1, one launch (start us, length us, event | category | flops | bytes accessed | tf_op | source)
XLA Modules:
  0.0 46.0 jit_solution(14531458685393243533)
XLA Ops:
  0.6 44.5 %shard_map.174 = (bf16[7,7,768]{2,1,0:T(8,128)(2,1)S(1)}, bf16[14,14,384]{2,1,0:T(8,128)(2,1)S(1)}, f32[16,128]{1,0:T(8,128)S(1)}) custom-call(bf16[14,14,384]{2,1,0:T(8,128)(2,1)} %bitcast.3, bf16[7,7,768]{2,1,0:T(8,128)(2,1)} %bitcast.4, f32[12,169]{1,0:T(8,128)} %bitcast.5, bf16[384,1152]{1,0:T(8,128)(2,1)} %refs_3_.1, bf16[384,384]{1,0:T(8,128)(2,1)} %refs_4_.1, ...), custom_call_target="tpu_custom_call" | custom-call | tf_op jit(solution)/shard_map/pallas_call | solution.py:754
  45.2 0.8 %shard_map.175 = (bf16[1,7,7,768]{3,2,1,0:T(8,128)(2,1)}, bf16[1,14,14,384]{3,2,1,0:T(8,128)(2,1)}, f32[864]{0:T(1024)}, f32[288]{0:T(512)}) custom-call(bf16[7,7,768]{2,1,0:T(8,128)(2,1)S(1)} %get-tuple-element.7.merged_in, bf16[14,14,384]{2,1,0:T(8,128)(2,1)S(1)} %get-tuple-element.8.grad_in, f32[16,128]{1,0:T(8,128)S(1)} %get-tuple-element.9.share), custom_call_target="tpu_custom_call" | custom-call | tf_op jit(solution)/shard_map/pallas_call | solution.py:772

commit v6 on v5

--- a/solution.py
+++ b/solution.py
@@ -631,14 +631,14 @@
     start_first(0)
     scores_back(0, 1)
     start_first(1)
+    start_core(3, mm(left_r[...], proj_grad[:, C : 2 * C]))
     start_core(2, mm(left_r[...], proj_grad[:, 0:C]))
-    start_core(3, mm(left_r[...], proj_grad[:, C : 2 * C]))
     east_grad = mm_t(proj_grad[192:256], w_attend[...])
     east_grad = normalize_back(normed_east[...], std_east[...], east_grad)
     ex_send[3] = east_grad.astype(BF)
     exchange(3, east_id).start()
+    start_first(3)
     start_first(2)
-    start_first(3)
     copies["to_window_t"].wait()
     own_proj = mm(to_window_t[:, 0:192], proj_grad[0:192]).astype(BF)
     own_grad = mm_t(own_proj, w_attend[...])

time: 46.1 us -> 46.1 us (level)
  no operation moved by 1% of the time
where the time goes in v6:
time: 46.1 us; the launch traced here: 46 us
  Pallas kernels  45.4 us (98%)
  between operations  0.64 us (1%)
    pallas_call x1, Pallas kernels, local_call(): pl.pallas_call(functools.partial(kernel, scatter), out_shape=(pltpu.VMEM(...  44.6 us

profile of v6, /device:TPU:1, one launch (start us, length us, event | category | flops | bytes accessed | tf_op | source)
XLA Modules:
  0.0 46.0 jit_solution(6771636985844172963)
XLA Ops:
  0.6 44.6 %shard_map.174 = (bf16[7,7,768]{2,1,0:T(8,128)(2,1)S(1)}, bf16[14,14,384]{2,1,0:T(8,128)(2,1)S(1)}, f32[16,128]{1,0:T(8,128)S(1)}) custom-call(bf16[14,14,384]{2,1,0:T(8,128)(2,1)} %bitcast.3, bf16[7,7,768]{2,1,0:T(8,128)(2,1)} %bitcast.4, f32[12,169]{1,0:T(8,128)} %bitcast.5, bf16[384,1152]{1,0:T(8,128)(2,1)} %refs_3_.1, bf16[384,384]{1,0:T(8,128)(2,1)} %refs_4_.1, ...), custom_call_target="tpu_custom_call" | custom-call | tf_op jit(solution)/shard_map/pallas_call | solution.py:754
  45.2 0.8 %shard_map.175 = (bf16[1,7,7,768]{3,2,1,0:T(8,128)(2,1)}, bf16[1,14,14,384]{3,2,1,0:T(8,128)(2,1)}, f32[864]{0:T(1024)}, f32[288]{0:T(512)}) custom-call(bf16[7,7,768]{2,1,0:T(8,128)(2,1)S(1)} %get-tuple-element.7.merged_in, bf16[14,14,384]{2,1,0:T(8,128)(2,1)S(1)} %get-tuple-element.8.grad_in, f32[16,128]{1,0:T(8,128)S(1)} %get-tuple-element.9.share), custom_call_target="tpu_custom_call" | custom-call | tf_op jit(solution)/shard_map/pallas_call | solution.py:772
